TPU v7x, 32 devices: a whole 2x2x4 slice. The times are simulated.
32 devices in a mesh: wave: 16 (over z, x, core), lev: 2 (over y).
Axes of the slice: x: 2, y: 2, z: 4, core: 2. Of those that a mesh axis runs over, the one named last changes fastest.
Arguments:
- spin_tendency: bfloat16 [32, 2, 136, 768], P('wave', None, 'lev'), may hold values from -6 to 6
- spreading_source: bfloat16 [32, 2, 136, 768], P('wave', None, 'lev'), may hold values from -6 to 6
- heat_source: bfloat16 [32, 2, 136, 768], P('wave', None, 'lev'), may hold values from -6 to 6
- helmholtz_inverses: bfloat16 [2, 384, 136, 136], P('lev', 'wave'), may hold values from -0.5 to 0.5
- heat_spreading_coupler: bfloat16 [136, 136], replicated, may hold values from -0.5 to 0.5
- smoothing_strengths: float32 [136], replicated, may hold values from 0.5 to 30
- azimuthal_order_list: int32 [32], P('wave'), may hold values from 0 to 767
Outputs:
- vorticity_new: bfloat16 [32, 2, 136, 768], P('wave', None, 'lev')
- divergence_new: bfloat16 [32, 2, 136, 768], P('wave', None, 'lev')
- temperature_new: bfloat16 [32, 2, 136, 768], P('wave', None, 'lev')
All inputs are finite; a program needn't handle non-finite values.
Results may differ from a plain program's by a relative error of at most 0.0075.
Values may be sent and summed in bfloat16 or wider, within the bound.
A program may use at most 64 MiB of HBM per device.

v0:
```python
import jax
import jax.numpy as jnp
from jax import lax
from jax.sharding import PartitionSpec as P


def damping_table(level_gain, wavenumbers, total_n):
    scaled = (wavenumbers * (wavenumbers + 1)).astype(jnp.float32) / jnp.float32(
        (total_n - 1) * total_n
    )
    return 1.0 / (1.0 + level_gain[:, None] * scaled[None, :] ** 2)


def on_device(
    spin_tendency,
    spreading_source,
    heat_source,
    helmholtz_inverses,
    heat_spreading_coupler,
    smoothing_strengths,
    azimuthal_order_list,
):
    lev_count = lax.axis_size("lev")
    lev_index = lax.axis_index("lev")
    row_count, part_count, lev_local, total_n = spreading_source.shape
    block_n = total_n // lev_count
    layer_count = lev_local * lev_count
    flat_rows = row_count * part_count
    empty_placeholder = jnp.zeros((), jnp.bfloat16)
    rhs_div = lax.all_to_all(spreading_source, "lev", split_axis=3, concat_axis=2, tiled=True)
    stacked = rhs_div.reshape(flat_rows, layer_count, block_n)
    gathered = lax.all_gather(helmholtz_inverses, "wave", axis=1, tiled=True)
    solved_full = jnp.einsum(
        "jkp,bpj->bkj", gathered[0], stacked, preferred_element_type=jnp.float32
    )
    answer_fields = solved_full.astype(jnp.bfloat16)
    coupled = jnp.einsum(
        "om,dms->dos", heat_spreading_coupler, answer_fields, preferred_element_type=jnp.float32
    ).astype(jnp.bfloat16)
    solved_rows = answer_fields.reshape(row_count, part_count, layer_count, block_n)
    coupled_rows = coupled.reshape(row_count, part_count, layer_count, block_n)
    spreading_updated, coupled_out = (
        lax.all_to_all(solved_rows, "lev", split_axis=2, concat_axis=3, tiled=True),
        lax.all_to_all(coupled_rows, "lev", split_axis=2, concat_axis=3, tiled=True),
    )
    heat_updated = (heat_source.astype(jnp.float32) - coupled_out.astype(jnp.float32)).astype(
        jnp.bfloat16
    )
    level_gain = lax.dynamic_slice_in_dim(smoothing_strengths, lev_index * lev_local, lev_local)
    damping = damping_table(level_gain, jnp.arange(total_n, dtype=jnp.int32), total_n)
    spin_updated = (spin_tendency.astype(jnp.float32) * damping[None, None]).astype(jnp.bfloat16)
    interior_slice = (
        jnp.arange(total_n, dtype=jnp.int32)[None, :] >= azimuthal_order_list[:, None]
    )[:, None, None, :]
    return (
        jnp.where(interior_slice, spin_updated, empty_placeholder),
        jnp.where(interior_slice, spreading_updated, empty_placeholder),
        jnp.where(interior_slice, heat_updated, empty_placeholder),
    )


def solution(mesh):
    return jax.shard_map(
        on_device,
        mesh=mesh,
        in_specs=(
            P("wave", None, "lev", None),
            P("wave", None, "lev", None),
            P("wave", None, "lev", None),
            P("lev", "wave", None, None),
            P(),
            P(),
            P("wave"),
        ),
        out_specs=(
            P("wave", None, "lev", None),
            P("wave", None, "lev", None),
            P("wave", None, "lev", None),
        ),
        check_vma=False,
    )
```

profile of v0, /device:TPU:0, one launch (start us, length us, event | category | flops | bytes accessed | tf_op | source)
XLA Modules:
  0.0 194.8 jit_solution(4959519182896049180)
XLA Ops:
  7.2 0.0 copy-start
  7.2 0.0 all-gather.2.cloned.1.call-start
  7.2 0.7 all-gather.2.cloned.1.call-update
  7.9 3.6 %copy.68 = bf16[2,2,68,768]{2,1,0,3:T(2,128)(2,1)} copy(bf16[2,2,68,768]{3,1,2,0:T(2,128)(2,1)} %param.8) | data formatting | bytes 835584 | tf_op args[1]
  11.5 4.3 %all-to-all-start = ((bf16[2,2,68,768]{2,1,0,3:T(2,128)(2,1)}), bf16[2,2,68,768]{2,1,0,3:T(2,128)(2,1)S(1)}, u32[]{:S(2)}, u32[]{:S(2)}) async-start(bf16[2,2,68,768]{2,1,0,3:T(2,128)(2,1)} %copy.68), calls=%async_computation | async-start | bytes 1572864 | tf_op jit(solution)/shard_map/all_to_all | solution.py:30
  15.7 0.8 dynamic_slice.3
  16.5 0.1 add_divide_fusion
  16.6 10.7 %all-to-all-done = bf16[2,2,68,768]{2,1,0,3:T(2,128)(2,1)S(1)} async-done(((bf16[2,2,68,768]{2,1,0,3:T(2,128)(2,1)}), bf16[2,2,68,768]{2,1,0,3:T(2,128)(2,1)S(1)}, u32[]{:S(2)}, u32[]{:S(2)}) %all-to-all-start) | async-done | bytes 417824 | tf_op jit(solution)/shard_map/all_to_all | solution.py:30
  27.3 0.7 copy.69
  28.0 0.0 copy-start.3
  28.0 0.1 reshape.75
  28.1 0.9 copy.71
  29.0 0.0 copy-start.1
  29.0 0.0 copy-start.2
  29.0 119.3 %all-gather.2.cloned.1.call-done = bf16[1,384,136,136]{3,2,0,1:T(8,128)(2,1)} async-done(((bf16[1,24,136,136]{3,2,0,1:T(8,128)(2,1)}), bf16[1,384,136,136]{3,2,0,1:T(8,128)(2,1)}) %all-gather.2.cloned.1.call-update) | async-done | bytes 14204944 | tf_op jit(solution)/shard_map/all_gather | solution.py:32
  148.3 12.1 %fusion.5 = bf16[4,136,384]{1,0,2:T(4,128)(2,1)S(1)} fusion(bf16[4,136,384]{1,0,2:T(4,128)(2,1)S(1)} %copy.71, bf16[1,384,136,136]{3,2,0,1:T(8,128)(2,1)} %all-gather.2.cloned.1.call-done), kind=kOutput, calls=%fused_computation.3 | convolution fusion | flops 57028608 | bytes 15040512 | tf_op jit(solution)/shard_map/jkp,bpj->bkj/dot_general | solution.py:33
  160.4 0.9 copy.72
  161.3 0.0 copy-done
  161.3 0.3 convolution_convert_fusion
  161.6 1.1 copy.78
  162.7 3.5 %all-to-all-start.2 = ((bf16[2,2,136,384]{3,1,0,2:T(2,128)(2,1)}), bf16[2,2,136,384]{3,1,0,2:T(2,128)(2,1)S(1)}, u32[]{:S(2)}, u32[]{:S(2)}) async-start(bf16[2,2,136,384]{3,1,0,2:T(2,128)(2,1)} %copy.78), calls=%async_computation.2 | async-start | bytes 835584 | tf_op jit(solution)/shard_map/all_to_all | solution.py:44
  166.2 0.0 copy-done.3
  166.2 0.1 iota_compare_fusion
  166.2 1.1 copy.73
  167.3 6.3 %all-to-all-done.2 = bf16[2,2,136,384]{3,1,0,2:T(2,128)(2,1)S(1)} async-done(((bf16[2,2,136,384]{3,1,0,2:T(2,128)(2,1)}), bf16[2,2,136,384]{3,1,0,2:T(2,128)(2,1)S(1)}, u32[]{:S(2)}, u32[]{:S(2)}) %all-to-all-start.2) | async-done | bytes 417824 | tf_op jit(solution)/shard_map/all_to_all | solution.py:44
  173.7 3.5 %all-to-all-start.1 = ((bf16[2,2,136,384]{3,1,0,2:T(2,128)(2,1)}), bf16[2,2,136,384]{3,1,0,2:T(2,128)(2,1)S(1)}, u32[]{:S(2)}, u32[]{:S(2)}) async-start(bf16[2,2,136,384]{3,1,0,2:T(2,128)(2,1)} %copy.73), calls=%async_computation.1 | async-start | bytes 835584 | tf_op jit(solution)/shard_map/all_to_all | solution.py:43
  177.2 0.1 copy_convert_fusion
  177.2 0.4 copy.80
  177.7 0.4 copy.81
  178.1 0.7 reshape.78
  178.8 5.0 %all-to-all-done.1 = bf16[2,2,136,384]{3,1,0,2:T(2,128)(2,1)S(1)} async-done(((bf16[2,2,136,384]{3,1,0,2:T(2,128)(2,1)}), bf16[2,2,136,384]{3,1,0,2:T(2,128)(2,1)S(1)}, u32[]{:S(2)}, u32[]{:S(2)}) %all-to-all-start.1) | async-done | bytes 417824 | tf_op jit(solution)/shard_map/all_to_all | solution.py:43
  183.8 0.3 copy.75
  184.1 0.3 all_to_all.37
  184.4 0.0 copy-done.1
  184.4 0.0 copy-done.2
  184.4 0.3 fusion.9
  184.8 1.1 copy.82
  185.8 1.1 copy.83
  186.9 1.1 copy.84
  (1 shorter events, 0.0 us)
Async XLA Ops:
  7.2 154.2 %copy-start = (bf16[136,136]{1,0:T(8,128)(2,1)S(1)}, bf16[136,136]{1,0:T(8,128)(2,1)}, u32[]{:S(2)}) copy-start(bf16[136,136]{1,0:T(8,128)(2,1)} %param.11) | copy-start | bytes 110980
  7.2 141.1 %all-gather.2.cloned.1.call-start = ((), (), s32[]{:S(2)}) async-start(), calls=%async_computation.3 | async-start | bytes 28409856 | tf_op jit(solution)/shard_map/all_gather | solution.py:32
  11.5 15.8 %all-to-all-start = ((bf16[2,2,68,768]{2,1,0,3:T(2,128)(2,1)}), bf16[2,2,68,768]{2,1,0,3:T(2,128)(2,1)S(1)}, u32[]{:S(2)}, u32[]{:S(2)}) async-start(bf16[2,2,68,768]{2,1,0,3:T(2,128)(2,1)} %copy.68), calls=%async_computation | async-start | bytes 1572864 | tf_op jit(solution)/shard_map/all_to_all | solution.py:30
  28.0 138.2 %copy-start.3 = (s32[2]{0:T(128)S(1)}, s32[2]{0:T(128)}, u32[]{:S(2)}) copy-start(s32[2]{0:T(128)} %param.13) | copy-start | bytes 28
  29.0 155.5 %copy-start.1 = (bf16[2,2,68,768]{3,1,2,0:T(2,128)(2,1)S(1)}, bf16[2,2,68,768]{3,1,2,0:T(2,128)(2,1)}, u32[]{:S(2)}) copy-start(bf16[2,2,68,768]{3,1,2,0:T(2,128)(2,1)} %param.9) | copy-start | bytes 1253380
  29.0 155.5 %copy-start.2 = (bf16[2,2,68,768]{3,1,2,0:T(2,128)(2,1)S(1)}, bf16[2,2,68,768]{3,1,2,0:T(2,128)(2,1)}, u32[]{:S(2)}) copy-start(bf16[2,2,68,768]{3,1,2,0:T(2,128)(2,1)} %param.7) | copy-start | bytes 1253380
  162.7 11.0 %all-to-all-start.2 = ((bf16[2,2,136,384]{3,1,0,2:T(2,128)(2,1)}), bf16[2,2,136,384]{3,1,0,2:T(2,128)(2,1)S(1)}, u32[]{:S(2)}, u32[]{:S(2)}) async-start(bf16[2,2,136,384]{3,1,0,2:T(2,128)(2,1)} %copy.78), calls=%async_computation.2 | async-start | bytes 835584 | tf_op jit(solution)/shard_map/all_to_all | solution.py:44
  173.7 10.1 %all-to-all-start.1 = ((bf16[2,2,136,384]{3,1,0,2:T(2,128)(2,1)}), bf16[2,2,136,384]{3,1,0,2:T(2,128)(2,1)S(1)}, u32[]{:S(2)}, u32[]{:S(2)}) async-start(bf16[2,2,136,384]{3,1,0,2:T(2,128)(2,1)} %copy.73), calls=%async_computation.1 | async-start | bytes 835584 | tf_op jit(solution)/shard_map/all_to_all | solution.py:43
Sparse Core Ops, SparseCore 0:
  9.6 138.6 all-gather.1
where the time goes:
time: 195 us
  waiting for transfers between devices  142 us (73%)
  local copies, waits for them, and re-layouts  14.3 us (7%)
  between operations  14.2 us (7%)
  matrix products  12.4 us (6%)
  starting transfers between devices  11.2 us (6%)
    all_gather x1, waiting for transfers between devices, on_device(): gathered = lax.all_gather(helmholtz_inverses, 'wave', axis=1, tiled=True)  119 us
    dot_general x1, matrix products, on_device(): jnp.einsum('jkp,bpj->bkj', gathered[0], stacked, preferred_element_type=j...  12.1 us
    all_to_all x1, waiting for transfers between devices, on_device(): lax.all_to_all(spreading_source, 'lev', split_axis=3, concat_axis=2, tile...  10.7 us
    unnamed x12, local copies, waits for them, and re-layouts  6.83 us
    all_to_all x1, waiting for transfers between devices, on_device(): lax.all_to_all(coupled_rows, 'lev', split_axis=2, concat_axis=3, tiled=True)  6.35 us
    all_to_all x1, waiting for transfers between devices, on_device(): lax.all_to_all(solved_rows, 'lev', split_axis=2, concat_axis=3, tiled=True)  5.03 us
    all_to_all x1, starting transfers between devices, on_device(): lax.all_to_all(spreading_source, 'lev', split_axis=3, concat_axis=2, tile...  4.26 us
  transfers between devices with their start and end apart: 4, of which 4 were waited for; matrix products, arithmetic and copies ran while one was open for 5% of the time, Pallas kernels for 0%

commit v1 on v0

--- a/solution.py
+++ b/solution.py
@@ -27,22 +27,26 @@
     layer_count = lev_local * lev_count
     flat_rows = row_count * part_count
     empty_placeholder = jnp.zeros((), jnp.bfloat16)
+    wave_count = lax.axis_size("wave")
+    local_n = block_n // wave_count
     rhs_div = lax.all_to_all(spreading_source, "lev", split_axis=3, concat_axis=2, tiled=True)
-    stacked = rhs_div.reshape(flat_rows, layer_count, block_n)
-    gathered = lax.all_gather(helmholtz_inverses, "wave", axis=1, tiled=True)
-    solved_full = jnp.einsum(
-        "jkp,bpj->bkj", gathered[0], stacked, preferred_element_type=jnp.float32
-    )
-    answer_fields = solved_full.astype(jnp.bfloat16)
+    outgoing = rhs_div.reshape(flat_rows, layer_count, wave_count, local_n).transpose(2, 3, 0, 1)
+    outgoing = outgoing.reshape(wave_count, local_n, flat_rows * layer_count)
+    columns = lax.all_to_all(outgoing, "wave", split_axis=0, concat_axis=0, tiled=True)
+    columns = columns.reshape(wave_count, local_n, flat_rows, layer_count)
+    solved_columns = jnp.einsum(
+        "jkp,wjcp->wjck", helmholtz_inverses[0], columns, preferred_element_type=jnp.float32
+    ).astype(jnp.bfloat16)
+    solved_columns = solved_columns.reshape(wave_count, local_n, flat_rows * layer_count)
+    returned = lax.all_to_all(solved_columns, "wave", split_axis=0, concat_axis=0, tiled=True)
+    answer_fields = returned.reshape(block_n, flat_rows, layer_count).transpose(1, 2, 0)
     coupled = jnp.einsum(
         "om,dms->dos", heat_spreading_coupler, answer_fields, preferred_element_type=jnp.float32
     ).astype(jnp.bfloat16)
-    solved_rows = answer_fields.reshape(row_count, part_count, layer_count, block_n)
-    coupled_rows = coupled.reshape(row_count, part_count, layer_count, block_n)
-    spreading_updated, coupled_out = (
-        lax.all_to_all(solved_rows, "lev", split_axis=2, concat_axis=3, tiled=True),
-        lax.all_to_all(coupled_rows, "lev", split_axis=2, concat_axis=3, tiled=True),
-    )
+    both = jnp.stack([answer_fields, coupled])
+    both = lax.all_to_all(both, "lev", split_axis=2, concat_axis=3, tiled=True)
+    both = both.reshape(2, row_count, part_count, lev_local, total_n)
+    spreading_updated, coupled_out = both[0], both[1]
     heat_updated = (heat_source.astype(jnp.float32) - coupled_out.astype(jnp.float32)).astype(
         jnp.bfloat16
     )

time: 195 us -> 88.8 us (0.46)
  waiting for transfers between devices: 142 us -> 24.6 us
  blocking collectives: 0 us -> 34.4 us
  between operations: 14.2 us -> 0.83 us
  matrix products: 12.4 us -> 0.91 us
  starting transfers between devices: 11.2 us -> 7.66 us
  other arithmetic: 0.57 us -> 3.5 us
  local copies, waits for them, and re-layouts: 14.3 us -> 16.3 us
    all_gather x1 -> x0, waiting for transfers between devices: 119 us -> none  [on_device(): gathered = lax.all_gather(helmholtz_inverses, 'wave', axis=1, tiled=True)]
    all_to_all x0 -> x2, blocking collectives: none -> 34.4 us  [the longest x1 19.6 us: on_device(): lax.all_to_all(outgoing, 'wave', split_axis=0, concat_axis=0, tiled=True)]
    dot_general x1, matrix products: 12.1 us -> 0.65 us  [on_device(): jnp.einsum('jkp,wjcp->wjck', helmholtz_inverses[0], columns, preferred_el...]
    all_to_all x3 -> x2, starting transfers between devices: 11.2 us -> 7.66 us  [the longest x1 4.12 us: on_device(): lax.all_to_all(solved_columns, 'wave', split_axis=0, concat_axis=0, tiled...]
    all_to_all x3 -> x2, waiting for transfers between devices: 22.1 us -> 24.6 us  [the longest x1 13.6 us: on_device(): lax.all_to_all(solved_columns, 'wave', split_axis=0, concat_axis=0, tiled...]
    reshape x4 -> x6, local copies, waits for them, and re-layouts: 3.09 us -> 4.12 us  [the longest x2 1.39 us: on_device(): returned.reshape(block_n, flat_rows, layer_count).transpose(1, 2, 0)]
  transfers between devices with their start and end apart: 4 -> 2, of which waited for: 4 -> 2; matrix products, arithmetic and copies ran while one was open for 5% -> 1% of each run, Pallas kernels for 0% -> 0%
where the time goes in v1:
time: 88.8 us; the launch traced here: 88.3 us
  blocking collectives  34.4 us (39%)
  waiting for transfers between devices  24.6 us (28%)
  local copies, waits for them, and re-layouts  16.3 us (18%)
  starting transfers between devices  7.66 us (9%)
  other arithmetic  3.5 us (4%)
  matrix products  0.91 us (1%)
    all_to_all x1, blocking collectives, on_device(): lax.all_to_all(outgoing, 'wave', split_axis=0, concat_axis=0, tiled=True)  19.6 us
    all_to_all x1, blocking collectives, on_device(): lax.all_to_all(spreading_source, 'lev', split_axis=3, concat_axis=2, tile...  14.8 us
    all_to_all x1, waiting for transfers between devices, on_device(): lax.all_to_all(solved_columns, 'wave', split_axis=0, concat_axis=0, tiled...  13.6 us
    all_to_all x1, waiting for transfers between devices, on_device(): both = lax.all_to_all(both, 'lev', split_axis=2, concat_axis=3, tiled=True)  11 us
    unnamed x12, local copies, waits for them, and re-layouts  6.1 us
    all_to_all x1, starting transfers between devices, on_device(): lax.all_to_all(solved_columns, 'wave', split_axis=0, concat_axis=0, tiled...  4.12 us
    all_to_all x1, starting transfers between devices, on_device(): both = lax.all_to_all(both, 'lev', split_axis=2, concat_axis=3, tiled=True)  3.54 us
  transfers between devices with their start and end apart: 2, of which 2 were waited for; matrix products, arithmetic and copies ran while one was open for 1% of the time, Pallas kernels for 0%

profile of v1, /device:TPU:0, one launch (start us, length us, event | category | flops | bytes accessed | tf_op | source)
XLA Modules:
  0.0 88.3 jit_solution(10291500777090711552)
XLA Ops:
  0.6 0.0 copy-start
  0.6 2.8 %copy.51 = bf16[2,2,68,768]{2,1,0,3:T(2,128)(2,1)S(1)} copy(bf16[2,2,68,768]{3,1,2,0:T(2,128)(2,1)} %param.8) | data formatting | bytes 835584 | tf_op args[1]
  3.5 14.8 %all_to_all.40 = bf16[2,2,68,768]{2,1,0,3:T(2,128)(2,1)S(1)} all-to-all(bf16[2,2,68,768]{2,1,0,3:T(2,128)(2,1)S(1)} %copy.51), channel_id=1, replica_groups=mesh['wave'=16,'lev'=2] {'lev'}, dimensions={3} | all-to-all | bytes 835584 | tf_op jit(solution)/shard_map/all_to_all | solution.py:32
  18.3 0.8 copy.71
  19.2 0.4 reshape.85
  19.6 0.6 copy.53
  20.2 0.5 reshape.86
  20.7 19.6 %all_to_all.41 = bf16[16,24,544]{2,1,0:T(8,128)(2,1)S(1)} all-to-all(bf16[16,24,544]{2,1,0:T(8,128)(2,1)S(1)} %reshape.86), channel_id=1, replica_groups=mesh['wave'=16,'lev'=2] {'wave'}, dimensions={0} | all-to-all | bytes 835584 | tf_op jit(solution)/shard_map/all_to_all | solution.py:35
  40.3 0.5 reshape.87
  40.8 0.0 copy-done
  40.8 0.7 fusion.5
  41.5 0.0 copy-start.3
  41.5 0.4 copy.55
  41.9 1.3 %reshape.88 = bf16[16,24,544]{2,1,0:T(8,128)(2,1)} reshape(bf16[16,24,4,136]{3,2,1,0:T(4,128)(2,1)S(1)} %copy.55) | data formatting | bytes 835584 | tf_op jit(solution)/shard_map/reshape | solution.py:40
  43.2 0.0 copy-start.1
  43.2 4.1 %all-to-all-start.2 = ((bf16[16,24,544]{2,1,0:T(8,128)(2,1)}), bf16[16,24,544]{2,1,0:T(8,128)(2,1)S(1)}, u32[]{:S(2)}, u32[]{:S(2)}) async-start(bf16[16,24,544]{2,1,0:T(8,128)(2,1)} %reshape.88), calls=%async_computation.2 | async-start | bytes 983040 | tf_op jit(solution)/shard_map/all_to_all | solution.py:41
  47.3 0.0 copy-done.3
  47.3 0.1 dynamic_slice.3
  47.4 13.6 %all-to-all-done.2 = bf16[16,24,544]{2,1,0:T(8,128)(2,1)S(1)} async-done(((bf16[16,24,544]{2,1,0:T(8,128)(2,1)}), bf16[16,24,544]{2,1,0:T(8,128)(2,1)S(1)}, u32[]{:S(2)}, u32[]{:S(2)}) %all-to-all-start.2) | async-done | bytes 417824 | tf_op jit(solution)/shard_map/all_to_all | solution.py:41
  61.1 0.5 reshape.89
  61.6 0.9 copy.56
  62.5 0.0 copy-done.1
  62.5 0.3 fusion.8
  62.8 0.1 pad_maximum_fusion
  62.9 0.0 copy-start.2
  62.9 1.2 %copy.57 = bf16[2,4,136,384]{3,1,0,2:T(4,128)(2,1)} copy(bf16[2,4,136,384]{3,2,1,0:T(8,128)(2,1)S(1)} %pad_maximum_fusion) | data formatting | bytes 1671168 | tf_op jit(solution)/shard_map/stack | solution.py:46
  64.1 3.5 %all-to-all-start.3 = ((bf16[2,4,136,384]{3,1,0,2:T(4,128)(2,1)}), bf16[2,4,136,384]{3,1,0,2:T(4,128)(2,1)S(1)}, u32[]{:S(2)}, u32[]{:S(2)}) async-start(bf16[2,4,136,384]{3,1,0,2:T(4,128)(2,1)} %copy.57), calls=%async_computation.3 | async-start | bytes 1671168 | tf_op jit(solution)/shard_map/all_to_all | solution.py:47
  67.6 0.0 copy-done.2
  67.7 0.1 iota_compare_fusion
  67.7 0.8 add_divide_fusion
  68.5 11.0 %all-to-all-done.3 = bf16[2,4,136,384]{3,1,0,2:T(4,128)(2,1)S(1)} async-done(((bf16[2,4,136,384]{3,1,0,2:T(4,128)(2,1)}), bf16[2,4,136,384]{3,1,0,2:T(4,128)(2,1)S(1)}, u32[]{:S(2)}, u32[]{:S(2)}) %all-to-all-start.3) | async-done | bytes 835616 | tf_op jit(solution)/shard_map/all_to_all | solution.py:47
  79.5 0.3 copy.58
  79.8 1.0 %slice_convert_fusion = (f32[1,4,68,2,384]{4,1,2,3,0:T(4,128)S(1)}, bf16[1,4,68,2,384]{4,1,2,3,0:T(4,128)(2,1)}) fusion(bf16[2,4,68,2,384]{4,1,2,3,0:T(4,128)(2,1)S(1)} %bitcast.35), kind=kLoop, calls=%fused_computation.14 | loop fusion | flops 208896 | bytes 2088960 | tf_op jit(solution)/shard_map/convert_element_type | solution.py:50
  80.8 0.4 copy.61
  81.2 0.7 reshape.90
  81.9 1.3 %copy.59 = bf16[1,4,68,2,384]{4,3,2,1,0:T(2,128)(2,1)S(1)} copy(bf16[1,4,68,2,384]{4,1,2,3,0:T(4,128)(2,1)} %get-tuple-element.16) | data formatting | bytes 835584 | tf_op jit(solution)/shard_map/slice | solution.py:49
  83.2 0.3 squeeze.8
  83.5 1.5 %fusion.11 = (bf16[2,2,68,768]{3,2,1,0:T(8,128)(2,1)S(1)}, bf16[2,2,68,768]{3,2,1,0:T(8,128)(2,1)S(1)}, bf16[2,2,68,768]{3,2,1,0:T(8,128)(2,1)S(1)}) fusion(f32[2,2,68,768]{3,2,1,0:T(8,128)S(1)} %reshape.90, bf16[2,2,68,768]{3,1,2,0:T(2,128)(2,1)} %param.9, pred[2,768]{1,0:T(4,128)(4,1)S(1)} %iota_compare_fusion, bf16[2,2,68,768]{3,2,1,0:T(8,128)(2,1)S(1)} %squeeze.8, ...), kind=kLoop, calls=%fused_computation.12 | loop fusion | flops 1880064 | bytes 3552768 | tf_op jit(solution)/shard_map/jit(_where)/select_n | solution.py:62
  85.1 1.1 %copy.64 = bf16[2,2,68,768]{3,1,2,0:T(2,128)(2,1)} copy(bf16[2,2,68,768]{3,2,1,0:T(8,128)(2,1)S(1)} %get-tuple-element.17) | data formatting | bytes 835584
  86.1 1.1 %copy.63 = bf16[2,2,68,768]{3,1,2,0:T(2,128)(2,1)} copy(bf16[2,2,68,768]{3,2,1,0:T(8,128)(2,1)S(1)} %get-tuple-element.18) | data formatting | bytes 835584
  87.2 1.1 %copy.62 = bf16[2,2,68,768]{3,1,2,0:T(2,128)(2,1)} copy(bf16[2,2,68,768]{3,2,1,0:T(8,128)(2,1)S(1)} %get-tuple-element.19) | data formatting | bytes 835584
  (1 shorter events, 0.0 us)
Async XLA Ops:
  0.6 40.2 %copy-start = (bf16[1,24,136,136]{3,2,1,0:T(8,128)(2,1)S(1)}, bf16[1,24,136,136]{3,2,1,0:T(8,128)(2,1)}, u32[]{:S(2)}) copy-start(bf16[1,24,136,136]{3,2,1,0:T(8,128)(2,1)} %param.10) | copy-start | bytes 2663428
  41.5 5.8 %copy-start.3 = (f32[136]{0:T(256)S(1)}, f32[136]{0:T(256)}, u32[]{:S(2)}) copy-start(f32[136]{0:T(256)} %param.12) | copy-start | bytes 1636
  43.2 19.3 %copy-start.1 = (bf16[136,136]{1,0:T(8,128)(2,1)S(1)}, bf16[136,136]{1,0:T(8,128)(2,1)}, u32[]{:S(2)}) copy-start(bf16[136,136]{1,0:T(8,128)(2,1)} %param.11) | copy-start | bytes 110980
  43.2 17.9 %all-to-all-start.2 = ((bf16[16,24,544]{2,1,0:T(8,128)(2,1)}), bf16[16,24,544]{2,1,0:T(8,128)(2,1)S(1)}, u32[]{:S(2)}, u32[]{:S(2)}) async-start(bf16[16,24,544]{2,1,0:T(8,128)(2,1)} %reshape.88), calls=%async_computation.2 | async-start | bytes 983040 | tf_op jit(solution)/shard_map/all_to_all | solution.py:41
  62.9 4.8 %copy-start.2 = (s32[2]{0:T(128)S(1)}, s32[2]{0:T(128)}, u32[]{:S(2)}) copy-start(s32[2]{0:T(128)} %param.13) | copy-start | bytes 28
  64.1 15.4 %all-to-all-start.3 = ((bf16[2,4,136,384]{3,1,0,2:T(4,128)(2,1)}), bf16[2,4,136,384]{3,1,0,2:T(4,128)(2,1)S(1)}, u32[]{:S(2)}, u32[]{:S(2)}) async-start(bf16[2,4,136,384]{3,1,0,2:T(4,128)(2,1)} %copy.57), calls=%async_computation.3 | async-start | bytes 1671168 | tf_op jit(solution)/shard_map/all_to_all | solution.py:47

commit v2 on v1

--- a/solution.py
+++ b/solution.py
@@ -1,7 +1,15 @@
+import functools
 import jax
 import jax.numpy as jnp
 from jax import lax
+from jax.experimental import pallas as pl
+from jax.experimental.pallas import tpu as pltpu
 from jax.sharding import PartitionSpec as P
+
+LANES = 128
+MESH = pl.DeviceIdType.MESH
+NT = (((1,), (1,)), ((), ()))
+TN = (((0,), (0,)), ((), ()))
 
 
 def damping_table(level_gain, wavenumbers, total_n):
@@ -11,22 +19,12 @@
     return 1.0 / (1.0 + level_gain[:, None] * scaled[None, :] ** 2)
 
 
-def on_device(
-    spin_tendency,
-    spreading_source,
-    heat_source,
-    helmholtz_inverses,
-    heat_spreading_coupler,
-    smoothing_strengths,
-    azimuthal_order_list,
-):
+def exchange_by_collectives(spreading_source, helmholtz_inverses, heat_spreading_coupler):
     lev_count = lax.axis_size("lev")
-    lev_index = lax.axis_index("lev")
     row_count, part_count, lev_local, total_n = spreading_source.shape
     block_n = total_n // lev_count
     layer_count = lev_local * lev_count
     flat_rows = row_count * part_count
-    empty_placeholder = jnp.zeros((), jnp.bfloat16)
     wave_count = lax.axis_size("wave")
     local_n = block_n // wave_count
     rhs_div = lax.all_to_all(spreading_source, "lev", split_axis=3, concat_axis=2, tiled=True)
@@ -47,6 +45,225 @@
     both = lax.all_to_all(both, "lev", split_axis=2, concat_axis=3, tiled=True)
     both = both.reshape(2, row_count, part_count, lev_local, total_n)
     spreading_updated, coupled_out = both[0], both[1]
+    return spreading_updated, coupled_out
+
+
+def f32_dot(left, right, dims):
+    return lax.dot_general(left, right, dims, preferred_element_type=jnp.float32)
+
+
+def exchange_kernel(
+    wave_count, lev_count, source, matrices, proj, solved_out, coupled_out,
+    halves, outgoing, columns, gathered, strided, returning, returned, results,
+    lev_send, lev_recv, wave_send, wave_recv, back_send, back_recv, last_send, last_recv,
+):
+    wave, lev = lax.axis_index("wave"), lax.axis_index("lev")
+    flat_rows, lev_local, total_n = source.shape
+    block_n = total_n // lev_count
+    local_n = block_n // wave_count
+    layer_count = lev_local * lev_count
+    extra = layer_count - LANES
+    main_lanes = flat_rows * LANES
+    wave_peers = [lax.rem(wave + s, wave_count) for s in range(1, wave_count)]
+    lev_peers = [lax.rem(lev + s, lev_count) for s in range(1, lev_count)]
+
+    barrier = pltpu.get_barrier_semaphore()
+    for peer in wave_peers:
+        pl.semaphore_signal(barrier, inc=1, device_id=(peer, lev), device_id_type=MESH)
+    for peer in lev_peers:
+        pl.semaphore_signal(barrier, inc=1, device_id=(wave, peer), device_id_type=MESH)
+    pl.semaphore_wait(barrier, wave_count + lev_count - 2)
+
+    def block_of(index):
+        return pl.ds(pl.multiple_of(index * block_n, LANES), block_n)
+
+    lev_copies = []
+    for s, peer in enumerate(lev_peers):
+        copy = pltpu.make_async_remote_copy(
+            src_ref=source.at[:, :, block_of(peer)], dst_ref=halves.at[s],
+            send_sem=lev_send.at[s], recv_sem=lev_recv.at[s],
+            device_id=(wave, peer), device_id_type=MESH,
+        )
+        copy.start()
+        lev_copies.append(copy)
+
+    def placed(row):
+        wide = proj[row]
+        first = wide[:, :LANES].astype(jnp.bfloat16)
+        rest = wide[:, LANES:]
+        out = []
+        for r in range(flat_rows):
+            rolled = pltpu.roll(rest, r * extra, 1) if r else rest
+            out.append(jnp.concatenate([first, rolled.astype(jnp.bfloat16)], axis=1))
+        return out
+
+    mine = placed(2 * lev)
+    mains = [f32_dot(source[r, :, block_of(lev)], mine[r], TN) for r in range(flat_rows)]
+    for s in range(lev_count - 1):
+        lev_copies[s].wait()
+        theirs = placed(2 * lax.rem(lev + lev_count - 1 - s, lev_count))
+        for r in range(flat_rows):
+            mains[r] += f32_dot(halves[s, r], theirs[r], TN)
+    rests = sum(m[:, LANES:] for m in mains)
+    packed = jnp.concatenate([m[:, :LANES] for m in mains] + [rests], axis=1)
+    outgoing[...] = packed.reshape(wave_count, local_n, main_lanes + LANES).astype(jnp.bfloat16)
+
+    def exchange(src, dst, send_sems, recv_sems):
+        copies = []
+        for s, peer in enumerate(wave_peers):
+            copy = pltpu.make_async_remote_copy(
+                src_ref=src.at[peer], dst_ref=dst.at[wave],
+                send_sem=send_sems.at[s], recv_sem=recv_sems.at[s],
+                device_id=(peer, lev), device_id_type=MESH,
+            )
+            copy.start()
+            copies.append(copy)
+        return copies
+
+    copies = exchange(outgoing, columns, wave_send, wave_recv)
+    columns[wave] = outgoing[wave]
+    for copy in copies:
+        copy.wait()
+    for w in range(wave_count):
+        for t in range(flat_rows + 1):
+            tile = columns[w, :, t * LANES:(t + 1) * LANES]
+            gathered[t, pl.ds(w * local_n, local_n), :] = tile.astype(jnp.float32)
+
+    lane = lax.broadcasted_iota(jnp.int32, (wave_count, LANES), 1)
+
+    def solve(j, carry):
+        rows = pl.ds(j, wave_count, stride=local_n)
+        rest = gathered[flat_rows, rows, :]
+        parts = []
+        for r in range(flat_rows):
+            rolled = pltpu.roll(rest, LANES - r * extra, 1) if r else rest
+            main = gathered[r, rows, :]
+            parts.append(jnp.concatenate([main, rolled], axis=1)[:, :layer_count])
+        stacked = jnp.concatenate(parts, axis=0).astype(jnp.bfloat16)
+        main = f32_dot(stacked, matrices[j, :LANES, :], NT)
+        last = f32_dot(stacked, matrices[j, layer_count - LANES:, :], NT)
+        rest = jnp.zeros((wave_count, LANES), jnp.float32)
+        for r in range(flat_rows):
+            strided[r, rows, :] = main[r * wave_count:(r + 1) * wave_count]
+            rolled = pltpu.roll(last[r * wave_count:(r + 1) * wave_count], (r + 1) * extra, 1)
+            keep = (lane >= r * extra) & (lane < (r + 1) * extra)
+            rest = jnp.where(keep, rolled, rest)
+        strided[flat_rows, rows, :] = rest
+        return carry
+
+    lax.fori_loop(0, local_n, solve, 0, unroll=4)
+    for w in range(wave_count):
+        for t in range(flat_rows + 1):
+            tile = strided[t, pl.ds(w * local_n, local_n), :]
+            returning[w, :, t * LANES:(t + 1) * LANES] = tile.astype(jnp.bfloat16)
+
+    copies = exchange(returning, returned, back_send, back_recv)
+    returned[wave] = returning[wave]
+    for copy in copies:
+        copy.wait()
+    back = returned[...].astype(jnp.float32).reshape(block_n, main_lanes + LANES)
+    back = back.astype(jnp.bfloat16)
+
+    def finish(row):
+        out = []
+        for r, weights in enumerate(placed(row)):
+            pair = jnp.concatenate(
+                [back[:, r * LANES:(r + 1) * LANES], back[:, main_lanes:]], axis=1
+            )
+            out.append(f32_dot(weights, pair, NT).astype(jnp.bfloat16))
+        return out
+
+    copies = []
+    for s, peer in enumerate(lev_peers):
+        for field, target in enumerate((solved_out, coupled_out)):
+            for r, value in enumerate(finish(2 * peer + field)):
+                results[s, field, r] = value
+            copy = pltpu.make_async_remote_copy(
+                src_ref=results.at[s, field], dst_ref=target.at[:, :, block_of(lev)],
+                send_sem=last_send.at[s, field], recv_sem=last_recv.at[s, field],
+                device_id=(wave, peer), device_id_type=MESH,
+            )
+            copy.start()
+            copies.append(copy)
+    for field, target in enumerate((solved_out, coupled_out)):
+        for r, value in enumerate(finish(2 * lev + field)):
+            target[r, :, block_of(lev)] = value
+    for copy in copies:
+        copy.wait()
+
+
+def exchange_by_kernel(spreading_source, helmholtz_inverses, heat_spreading_coupler):
+    lev_count, wave_count = lax.axis_size("lev"), lax.axis_size("wave")
+    row_count, part_count, lev_local, total_n = spreading_source.shape
+    block_n = total_n // lev_count
+    local_n = block_n // wave_count
+    layer_count = lev_local * lev_count
+    flat_rows = row_count * part_count
+    width = (flat_rows + 1) * LANES
+    proj = jnp.stack([jnp.eye(layer_count, dtype=jnp.float32), heat_spreading_coupler.astype(jnp.float32)])
+    proj = jnp.pad(proj, ((0, 0), (0, 0), (0, 2 * LANES - layer_count)))
+    proj = proj.reshape(2, lev_count, lev_local, 2 * LANES).transpose(1, 0, 2, 3)
+    proj = proj.reshape(2 * lev_count, lev_local, 2 * LANES)
+    vmem = pl.BlockSpec(memory_space=pltpu.VMEM)
+    field = jax.ShapeDtypeStruct((flat_rows, lev_local, total_n), jnp.bfloat16)
+    wire = pltpu.VMEM((wave_count, local_n, width), jnp.bfloat16)
+    wide = pltpu.VMEM((flat_rows + 1, block_n, LANES), jnp.float32)
+    dma = pltpu.SemaphoreType.DMA
+    solved, coupled = pl.pallas_call(
+        functools.partial(exchange_kernel, wave_count, lev_count),
+        out_shape=(field, field),
+        in_specs=[vmem] * 3,
+        out_specs=(vmem, vmem),
+        scratch_shapes=[
+            pltpu.VMEM((lev_count - 1, flat_rows, lev_local, block_n), jnp.bfloat16),
+            wire, wire, wide, wide, wire, wire,
+            pltpu.VMEM((lev_count - 1, 2, flat_rows, lev_local, block_n), jnp.bfloat16),
+            dma((lev_count - 1,)), dma((lev_count - 1,)),
+            dma((wave_count - 1,)), dma((wave_count - 1,)),
+            dma((wave_count - 1,)), dma((wave_count - 1,)),
+            dma((lev_count - 1, 2)), dma((lev_count - 1, 2)),
+        ],
+        compiler_params=pltpu.CompilerParams(
+            collective_id=0, has_side_effects=True, vmem_limit_bytes=48 * 2**20
+        ),
+    )(spreading_source.reshape(field.shape), helmholtz_inverses[0], proj)
+    shape = spreading_source.shape
+    return solved.reshape(shape), coupled.reshape(shape)
+
+
+def kernel_fits(source_shape, lev_count, wave_count):
+    row_count, part_count, lev_local, total_n = source_shape
+    block_n = total_n // lev_count
+    extra = lev_local * lev_count - LANES
+    return (
+        lev_count > 1
+        and wave_count > 1
+        and wave_count % 8 == 0
+        and block_n % LANES == 0
+        and block_n % (8 * wave_count) == 0
+        and extra > 0
+        and extra * row_count * part_count <= LANES
+    )
+
+
+def on_device(
+    spin_tendency,
+    spreading_source,
+    heat_source,
+    helmholtz_inverses,
+    heat_spreading_coupler,
+    smoothing_strengths,
+    azimuthal_order_list,
+):
+    lev_count, wave_count = lax.axis_size("lev"), lax.axis_size("wave")
+    lev_index = lax.axis_index("lev")
+    lev_local, total_n = spreading_source.shape[2:]
+    empty_placeholder = jnp.zeros((), jnp.bfloat16)
+    fits = kernel_fits(spreading_source.shape, lev_count, wave_count)
+    exchange = exchange_by_kernel if fits else exchange_by_collectives
+    spreading_updated, coupled_out = exchange(
+        spreading_source, helmholtz_inverses, heat_spreading_coupler
+    )
     heat_updated = (heat_source.astype(jnp.float32) - coupled_out.astype(jnp.float32)).astype(
         jnp.bfloat16
     )

time: 88.8 us -> 55.7 us (0.63)
  the two profiles are of different devices: /device:TPU:0 before, /device:TPU:30 now
where the time goes in v2:
time: 55.7 us; the launch traced here: 55.5 us
  Pallas kernels  48.5 us (87%)
  other arithmetic  4.09 us (7%)
  local copies, waits for them, and re-layouts  2.07 us (4%)
  between operations  0.75 us (1%)
    pallas_call x1, Pallas kernels, exchange_by_kernel(): pl.pallas_call(functools.partial(exchange_kernel, wave_count, lev_count),...  48.5 us
    select_n x1, other arithmetic, on_device(): jnp.where(interior_slice, heat_updated, empty_placeholder)  2.26 us
    unnamed x10, local copies, waits for them, and re-layouts  1.15 us

profile of v2, /device:TPU:30, one launch (start us, length us, event | category | flops | bytes accessed | tf_op | source)
XLA Modules:
  0.0 55.5 jit_solution(16898022965763705856)
XLA Ops:
  0.6 0.0 copy-start.1
  0.6 0.8 %dynamic_slice.3 = f32[68]{0:T(128)S(1)} dynamic-slice(f32[136]{0:T(256)} %param.12, s32[]{:T(128)S(6)} %select_n.13), dynamic_slice_sizes={68} | dynamic-slice | bytes 548 | tf_op jit(solution)/shard_map/dynamic_slice | solution.py:270
  1.4 0.7 %iota_compare_fusion.1 = pred[2,768]{1,0:T(4,128)(4,1)S(1)} fusion(s32[2]{0:T(128)} %param.13), kind=kLoop, calls=%fused_computation.12 | loop fusion | flops 1536 | bytes 1544 | tf_op jit(solution)/shard_map/ge | solution.py:274
  2.2 0.9 %bitcast_convert_fusion = f32[1,136,136]{2,1,0:T(8,128)S(1)} fusion(bf16[136,136]{1,0:T(8,128)(2,1)} %param.11), kind=kLoop, calls=%fused_computation.10 | loop fusion | flops 18496 | bytes 110976 | tf_op jit(solution)/shard_map/stack | solution.py:203
  3.1 0.0 copy-start
  3.1 0.1 copy.19
  3.3 0.1 pad.4.clone
  3.4 0.1 add_divide_fusion
  3.5 0.0 copy-done.1
  3.6 0.9 %copy-done = bf16[1,24,136,136]{3,2,1,0:T(8,128)(2,1)S(1)} copy-done((bf16[1,24,136,136]{3,2,1,0:T(8,128)(2,1)S(1)}, bf16[1,24,136,136]{3,2,1,0:T(8,128)(2,1)}, u32[]{:S(2)}) %copy-start) | copy-done | bytes 887832
  4.6 0.0 copy-start.2
  4.6 0.0 copy-start.3
  4.6 48.5 %shard_map.94 = (bf16[4,68,768]{2,1,0:T(8,128)(2,1)S(1)}, bf16[4,68,768]{2,1,0:T(8,128)(2,1)S(1)}) custom-call(bf16[4,68,768]{2,1,0:T(8,128)(2,1)S(1)} %bitcast.12, bf16[24,136,136]{2,1,0:T(8,128)(2,1)S(1)} %bitcast.13, f32[4,68,256]{2,1,0:T(8,128)S(1)} %bitcast.14), custom_call_target="tpu_custom_call" | custom-call | tf_op jit(solution)/shard_map/pallas_call | solution.py:212
  53.1 0.1 convert.3
  53.2 0.0 copy-done.2
  53.2 0.0 copy-done.3
  53.2 2.3 %broadcast_select_fusion = (bf16[2,2,68,768]{3,1,2,0:T(2,128)(2,1)}, bf16[2,2,68,768]{3,1,2,0:T(2,128)(2,1)}, bf16[2,2,68,768]{3,1,2,0:T(2,128)(2,1)}) fusion(pred[2,768]{1,0:T(4,128)(4,1)S(1)} %iota_compare_fusion.1, f32[2,2,68,768]{3,2,1,0:T(8,128)S(1)} %convert.3, bf16[2,2,68,768]{3,1,2,0:T(2,128)(2,1)S(1)} %copy-done.2, ...), kind=kLoop, calls=%fused_computation.3 | loop fusion | flops 1880064 | bytes 3552768 | tf_op jit(solution)/shard_map/jit(_where)/select_n | solution.py:279
  (5 shorter events, 0.1 us)
Async XLA Ops:
  0.6 2.9 %copy-start.1 = (bf16[2,2,68,768]{3,1,2,0:T(2,128)(2,1)S(1)}, bf16[2,2,68,768]{3,1,2,0:T(2,128)(2,1)}, u32[]{:S(2)}) copy-start(bf16[2,2,68,768]{3,1,2,0:T(2,128)(2,1)} %param.8) | copy-start | bytes 1253380
  3.1 1.4 %copy-start = (bf16[1,24,136,136]{3,2,1,0:T(8,128)(2,1)S(1)}, bf16[1,24,136,136]{3,2,1,0:T(8,128)(2,1)}, u32[]{:S(2)}) copy-start(bf16[1,24,136,136]{3,2,1,0:T(8,128)(2,1)} %param.10) | copy-start | bytes 2663428
  4.6 48.6 %copy-start.2 = (bf16[2,2,68,768]{3,1,2,0:T(2,128)(2,1)S(1)}, bf16[2,2,68,768]{3,1,2,0:T(2,128)(2,1)}, u32[]{:S(2)}) copy-start(bf16[2,2,68,768]{3,1,2,0:T(2,128)(2,1)} %param.9) | copy-start | bytes 1253380
  4.6 48.6 %copy-start.3 = (bf16[2,2,68,768]{3,1,2,0:T(2,128)(2,1)S(1)}, bf16[2,2,68,768]{3,1,2,0:T(2,128)(2,1)}, u32[]{:S(2)}) copy-start(bf16[2,2,68,768]{3,1,2,0:T(2,128)(2,1)} %param.7) | copy-start | bytes 1253380

commit v3 on v2

v3 whole, which is shorter than its diff:
```python
import functools
import jax
import jax.numpy as jnp
from jax import lax
from jax.experimental import pallas as pl
from jax.experimental.pallas import tpu as pltpu
from jax.sharding import PartitionSpec as P

LANES = 128
MESH = pl.DeviceIdType.MESH
NT = (((1,), (1,)), ((), ()))
TN = (((0,), (0,)), ((), ()))


def damping_table(level_gain, wavenumbers, total_n):
    scaled = (wavenumbers * (wavenumbers + 1)).astype(jnp.float32) / jnp.float32(
        (total_n - 1) * total_n
    )
    return 1.0 / (1.0 + level_gain[:, None] * scaled[None, :] ** 2)


def exchange_by_collectives(spreading_source, helmholtz_inverses, heat_spreading_coupler):
    lev_count = lax.axis_size("lev")
    row_count, part_count, lev_local, total_n = spreading_source.shape
    block_n = total_n // lev_count
    layer_count = lev_local * lev_count
    flat_rows = row_count * part_count
    wave_count = lax.axis_size("wave")
    local_n = block_n // wave_count
    rhs_div = lax.all_to_all(spreading_source, "lev", split_axis=3, concat_axis=2, tiled=True)
    outgoing = rhs_div.reshape(flat_rows, layer_count, wave_count, local_n).transpose(2, 3, 0, 1)
    outgoing = outgoing.reshape(wave_count, local_n, flat_rows * layer_count)
    columns = lax.all_to_all(outgoing, "wave", split_axis=0, concat_axis=0, tiled=True)
    columns = columns.reshape(wave_count, local_n, flat_rows, layer_count)
    solved_columns = jnp.einsum(
        "jkp,wjcp->wjck", helmholtz_inverses[0], columns, preferred_element_type=jnp.float32
    ).astype(jnp.bfloat16)
    solved_columns = solved_columns.reshape(wave_count, local_n, flat_rows * layer_count)
    returned = lax.all_to_all(solved_columns, "wave", split_axis=0, concat_axis=0, tiled=True)
    answer_fields = returned.reshape(block_n, flat_rows, layer_count).transpose(1, 2, 0)
    coupled = jnp.einsum(
        "om,dms->dos", heat_spreading_coupler, answer_fields, preferred_element_type=jnp.float32
    ).astype(jnp.bfloat16)
    both = jnp.stack([answer_fields, coupled])
    both = lax.all_to_all(both, "lev", split_axis=2, concat_axis=3, tiled=True)
    both = both.reshape(2, row_count, part_count, lev_local, total_n)
    spreading_updated, coupled_out = both[0], both[1]
    return spreading_updated, coupled_out


def f32_dot(left, right, dims):
    return lax.dot_general(left, right, dims, preferred_element_type=jnp.float32)


def chunk_rows(flat_rows):
    size = max(1, flat_rows // 2)
    return [range(r, min(r + size, flat_rows)) for r in range(0, flat_rows, size)]


def exchange_kernel(wave_count, lev_count, chunks, source, matrices, proj, solved_out, coupled_out, *scratch):
    count = len(chunks)
    halves, gathered, strided, results = scratch[:4]
    outgoing, columns, returning, returned = (
        scratch[4 + k * count:4 + (k + 1) * count] for k in range(4)
    )
    (lev_send, lev_recv, wave_send, wave_recv, back_send, back_recv, last_send, last_recv) = scratch[
        4 + 4 * count:
    ]
    wave, lev = lax.axis_index("wave"), lax.axis_index("lev")
    flat_rows, lev_local, total_n = source.shape
    block_n = total_n // lev_count
    local_n = block_n // wave_count
    groups = local_n // 8
    layer_count = lev_local * lev_count
    extra = layer_count - LANES
    wave_peers = [lax.rem(wave + s, wave_count) for s in range(1, wave_count)]
    lev_peers = [lax.rem(lev + s, lev_count) for s in range(1, lev_count)]

    barrier = pltpu.get_barrier_semaphore()
    for peer in wave_peers:
        pl.semaphore_signal(barrier, inc=1, device_id=(peer, lev), device_id_type=MESH)
    for peer in lev_peers:
        pl.semaphore_signal(barrier, inc=1, device_id=(wave, peer), device_id_type=MESH)
    pl.semaphore_wait(barrier, wave_count + lev_count - 2)

    def block_of(index):
        return pl.ds(pl.multiple_of(index * block_n, LANES), block_n)

    def rows_of(c):
        return pl.ds(chunks[c][0], len(chunks[c]))

    lev_copies = []
    for c in range(count):
        for s, peer in enumerate(lev_peers):
            copy = pltpu.make_async_remote_copy(
                src_ref=source.at[rows_of(c), :, block_of(peer)], dst_ref=halves.at[s, rows_of(c)],
                send_sem=lev_send.at[s, c], recv_sem=lev_recv.at[s, c],
                device_id=(wave, peer), device_id_type=MESH,
            )
            copy.start()
            lev_copies.append(copy)

    def shifted(tile, amount):
        amount = amount % LANES
        return pltpu.roll(tile, amount, 1) if amount else tile

    def placed(row, size):
        wide = proj[row]
        first = wide[:, :LANES].astype(jnp.bfloat16)
        rest = wide[:, LANES:]
        return [
            jnp.concatenate([first, shifted(rest, i * extra).astype(jnp.bfloat16)], axis=1)
            for i in range(size)
        ]

    def pack(mains, rest, step):
        rest = rest.reshape(wave_count, groups, 8, LANES)
        folded = rest[:, 0].reshape(wave_count * 8, LANES)
        for g in range(1, groups):
            folded += shifted(rest[:, g].reshape(wave_count * 8, LANES), g * step)
        pieces = [m.reshape(wave_count, local_n, LANES) for m in mains]
        pieces.append(folded.reshape(wave_count, 8, LANES))
        return jnp.concatenate(pieces, axis=1).astype(jnp.bfloat16)

    def unpack(wire, size):
        step = size * extra
        value = wire[...].astype(jnp.float32)
        mains = [
            value[:, i * local_n:(i + 1) * local_n].reshape(block_n, LANES) for i in range(size)
        ]
        folded = value[:, size * local_n:].reshape(wave_count * 8, LANES)
        rest = [
            shifted(folded, -g * step).reshape(wave_count, 1, 8, LANES) for g in range(groups)
        ]
        return mains, jnp.concatenate(rest, axis=1).reshape(block_n, LANES)

    def exchange(src, dst, send_sems, recv_sems, c):
        copies = []
        for s, peer in enumerate(wave_peers):
            copy = pltpu.make_async_remote_copy(
                src_ref=src[c].at[peer], dst_ref=dst[c].at[wave],
                send_sem=send_sems.at[s, c], recv_sem=recv_sems.at[s, c],
                device_id=(peer, lev), device_id_type=MESH,
            )
            copy.start()
            copies.append(copy)
        dst[c][wave] = src[c][wave]
        return copies

    lane = lax.broadcasted_iota(jnp.int32, (wave_count, LANES), 1)
    out_copies, back_copies, last_copies = [], [], []
    for c, chunk in enumerate(chunks):
        size = len(chunk)
        mine = placed(2 * lev, size)
        sums = [f32_dot(source[r, :, block_of(lev)], mine[i], TN) for i, r in enumerate(chunk)]
        for s in range(lev_count - 1):
            lev_copies[c * (lev_count - 1) + s].wait()
            theirs = placed(2 * lax.rem(lev + lev_count - 1 - s, lev_count), size)
            for i, r in enumerate(chunk):
                sums[i] += f32_dot(halves[s, r], theirs[i], TN)
        rest = sum(m[:, LANES:] for m in sums)
        outgoing[c][...] = pack([m[:, :LANES] for m in sums], rest, size * extra)
        out_copies.append(exchange(outgoing, columns, wave_send, wave_recv, c))

    for c, chunk in enumerate(chunks):
        size = len(chunk)
        for copy in out_copies[c]:
            copy.wait()
        mains, rest = unpack(columns[c], size)
        for i, main in enumerate(mains):
            gathered[i] = main
        gathered[size] = rest

        def solve(j, carry):
            rows = pl.ds(j, wave_count, stride=local_n)
            rest = gathered[size, rows, :]
            parts = []
            for i in range(size):
                both = [gathered[i, rows, :], shifted(rest, -i * extra)]
                parts.append(jnp.concatenate(both, axis=1)[:, :layer_count])
            stacked = jnp.concatenate(parts, axis=0).astype(jnp.bfloat16)
            main = f32_dot(stacked, matrices[j, :LANES, :], NT)
            last = f32_dot(stacked, matrices[j, layer_count - LANES:, :], NT)
            rest = jnp.zeros((wave_count, LANES), jnp.float32)
            for i in range(size):
                part = slice(i * wave_count, (i + 1) * wave_count)
                strided[i, rows, :] = main[part]
                keep = (lane >= i * extra) & (lane < (i + 1) * extra)
                rest = jnp.where(keep, shifted(last[part], (i + 1) * extra), rest)
            strided[size, rows, :] = rest
            return carry

        lax.fori_loop(0, local_n, solve, 0, unroll=4)
        returning[c][...] = pack([strided[i] for i in range(size)], strided[size], size * extra)
        back_copies.append(exchange(returning, returned, back_send, back_recv, c))

    for c, chunk in enumerate(chunks):
        size = len(chunk)
        for copy in back_copies[c]:
            copy.wait()
        mains, rest = unpack(returned[c], size)
        pairs = [jnp.concatenate([main, rest], axis=1).astype(jnp.bfloat16) for main in mains]

        def finish(row):
            return [
                f32_dot(weights, pair, NT).astype(jnp.bfloat16)
                for weights, pair in zip(placed(row, size), pairs)
            ]

        for s, peer in enumerate(lev_peers):
            for field, target in enumerate((solved_out, coupled_out)):
                for r, value in zip(chunk, finish(2 * peer + field)):
                    results[s, field, r] = value
                copy = pltpu.make_async_remote_copy(
                    src_ref=results.at[s, field, rows_of(c)],
                    dst_ref=target.at[rows_of(c), :, block_of(lev)],
                    send_sem=last_send.at[s, field, c], recv_sem=last_recv.at[s, field, c],
                    device_id=(wave, peer), device_id_type=MESH,
                )
                copy.start()
                last_copies.append(copy)
        for field, target in enumerate((solved_out, coupled_out)):
            for r, value in zip(chunk, finish(2 * lev + field)):
                target[r, :, block_of(lev)] = value
    for copy in last_copies:
        copy.wait()


def exchange_by_kernel(spreading_source, helmholtz_inverses, heat_spreading_coupler):
    lev_count, wave_count = lax.axis_size("lev"), lax.axis_size("wave")
    row_count, part_count, lev_local, total_n = spreading_source.shape
    block_n = total_n // lev_count
    local_n = block_n // wave_count
    layer_count = lev_local * lev_count
    flat_rows = row_count * part_count
    chunks = chunk_rows(flat_rows)
    longest = max(len(chunk) for chunk in chunks)
    proj = jnp.stack([jnp.eye(layer_count, dtype=jnp.float32), heat_spreading_coupler.astype(jnp.float32)])
    proj = jnp.pad(proj, ((0, 0), (0, 0), (0, 2 * LANES - layer_count)))
    proj = proj.reshape(2, lev_count, lev_local, 2 * LANES).transpose(1, 0, 2, 3)
    proj = proj.reshape(2 * lev_count, lev_local, 2 * LANES)
    vmem = pl.BlockSpec(memory_space=pltpu.VMEM)
    field = jax.ShapeDtypeStruct((flat_rows, lev_local, total_n), jnp.bfloat16)
    wires = [pltpu.VMEM((wave_count, len(c) * local_n + 8, LANES), jnp.bfloat16) for c in chunks]
    wide = pltpu.VMEM((longest + 1, block_n, LANES), jnp.float32)
    dma = pltpu.SemaphoreType.DMA
    lev_sems, wave_sems = dma((lev_count - 1, len(chunks))), dma((wave_count - 1, len(chunks)))
    last_sems = dma((lev_count - 1, 2, len(chunks)))
    solved, coupled = pl.pallas_call(
        functools.partial(exchange_kernel, wave_count, lev_count, chunks),
        out_shape=(field, field),
        in_specs=[vmem] * 3,
        out_specs=(vmem, vmem),
        scratch_shapes=[
            pltpu.VMEM((lev_count - 1, flat_rows, lev_local, block_n), jnp.bfloat16),
            wide, wide,
            pltpu.VMEM((lev_count - 1, 2, flat_rows, lev_local, block_n), jnp.bfloat16),
            *wires, *wires, *wires, *wires,
            lev_sems, lev_sems, wave_sems, wave_sems, wave_sems, wave_sems, last_sems, last_sems,
        ],
        compiler_params=pltpu.CompilerParams(
            collective_id=0, has_side_effects=True, vmem_limit_bytes=48 * 2**20
        ),
    )(spreading_source.reshape(field.shape), helmholtz_inverses[0], proj)
    shape = spreading_source.shape
    return solved.reshape(shape), coupled.reshape(shape)


def kernel_fits(source_shape, lev_count, wave_count):
    row_count, part_count, lev_local, total_n = source_shape
    block_n = total_n // lev_count
    extra = lev_local * lev_count - LANES
    return (
        lev_count > 1
        and wave_count > 1
        and wave_count % 8 == 0
        and block_n % LANES == 0
        and block_n % (8 * wave_count) == 0
        and extra > 0
        and extra * row_count * part_count * (block_n // (8 * wave_count)) <= LANES
    )


def on_device(
    spin_tendency,
    spreading_source,
    heat_source,
    helmholtz_inverses,
    heat_spreading_coupler,
    smoothing_strengths,
    azimuthal_order_list,
):
    lev_count, wave_count = lax.axis_size("lev"), lax.axis_size("wave")
    lev_index = lax.axis_index("lev")
    lev_local, total_n = spreading_source.shape[2:]
    empty_placeholder = jnp.zeros((), jnp.bfloat16)
    fits = kernel_fits(spreading_source.shape, lev_count, wave_count)
    exchange = exchange_by_kernel if fits else exchange_by_collectives
    spreading_updated, coupled_out = exchange(
        spreading_source, helmholtz_inverses, heat_spreading_coupler
    )
    heat_updated = (heat_source.astype(jnp.float32) - coupled_out.astype(jnp.float32)).astype(
        jnp.bfloat16
    )
    level_gain = lax.dynamic_slice_in_dim(smoothing_strengths, lev_index * lev_local, lev_local)
    damping = damping_table(level_gain, jnp.arange(total_n, dtype=jnp.int32), total_n)
    spin_updated = (spin_tendency.astype(jnp.float32) * damping[None, None]).astype(jnp.bfloat16)
    interior_slice = (
        jnp.arange(total_n, dtype=jnp.int32)[None, :] >= azimuthal_order_list[:, None]
    )[:, None, None, :]
    return (
        jnp.where(interior_slice, spin_updated, empty_placeholder),
        jnp.where(interior_slice, spreading_updated, empty_placeholder),
        jnp.where(interior_slice, heat_updated, empty_placeholder),
    )


def solution(mesh):
    return jax.shard_map(
        on_device,
        mesh=mesh,
        in_specs=(
            P("wave", None, "lev", None),
            P("wave", None, "lev", None),
            P("wave", None, "lev", None),
            P("lev", "wave", None, None),
            P(),
            P(),
            P("wave"),
        ),
        out_specs=(
            P("wave", None, "lev", None),
            P("wave", None, "lev", None),
            P("wave", None, "lev", None),
        ),
        check_vma=False,
    )
```

time: 55.7 us -> 48.5 us (0.87)
  the two profiles are of different devices: /device:TPU:30 before, /device:TPU:0 now
where the time goes in v3:
time: 48.5 us; the launch traced here: 47.8 us
  Pallas kernels  40.9 us (84%)
  other arithmetic  4.09 us (8%)
  local copies, waits for them, and re-layouts  2.07 us (4%)
  between operations  0.75 us (2%)
    pallas_call x1, Pallas kernels, exchange_by_kernel(): pl.pallas_call(functools.partial(exchange_kernel, wave_count, lev_count,...  40.9 us
    select_n x1, other arithmetic, on_device(): jnp.where(interior_slice, heat_updated, empty_placeholder)  2.26 us
    unnamed x10, local copies, waits for them, and re-layouts  1.15 us

profile of v3, /device:TPU:0, one launch (start us, length us, event | category | flops | bytes accessed | tf_op | source)
XLA Modules:
  0.0 47.8 jit_solution(601888023579585488)
XLA Ops:
  0.6 0.0 copy-start.1
  0.6 0.8 %dynamic_slice.3 = f32[68]{0:T(128)S(1)} dynamic-slice(f32[136]{0:T(256)} %param.12, s32[]{:T(128)S(6)} %select_n.13), dynamic_slice_sizes={68} | dynamic-slice | bytes 548 | tf_op jit(solution)/shard_map/dynamic_slice | solution.py:305
  1.4 0.7 %iota_compare_fusion.1 = pred[2,768]{1,0:T(4,128)(4,1)S(1)} fusion(s32[2]{0:T(128)} %param.13), kind=kLoop, calls=%fused_computation.12 | loop fusion | flops 1536 | bytes 1544 | tf_op jit(solution)/shard_map/ge | solution.py:309
  2.2 0.9 %bitcast_convert_fusion = f32[1,136,136]{2,1,0:T(8,128)S(1)} fusion(bf16[136,136]{1,0:T(8,128)(2,1)} %param.11), kind=kLoop, calls=%fused_computation.10 | loop fusion | flops 18496 | bytes 110976 | tf_op jit(solution)/shard_map/stack | solution.py:238
  3.1 0.0 copy-start
  3.1 0.1 copy.19
  3.3 0.1 pad.4.clone
  3.4 0.1 add_divide_fusion
  3.5 0.0 copy-done.1
  3.6 0.9 %copy-done = bf16[1,24,136,136]{3,2,1,0:T(8,128)(2,1)S(1)} copy-done((bf16[1,24,136,136]{3,2,1,0:T(8,128)(2,1)S(1)}, bf16[1,24,136,136]{3,2,1,0:T(8,128)(2,1)}, u32[]{:S(2)}) %copy-start) | copy-done | bytes 887832
  4.6 0.0 copy-start.2
  4.6 0.0 copy-start.3
  4.6 40.9 %shard_map.94 = (bf16[4,68,768]{2,1,0:T(8,128)(2,1)S(1)}, bf16[4,68,768]{2,1,0:T(8,128)(2,1)S(1)}) custom-call(bf16[4,68,768]{2,1,0:T(8,128)(2,1)S(1)} %bitcast.12, bf16[24,136,136]{2,1,0:T(8,128)(2,1)S(1)} %bitcast.13, f32[4,68,256]{2,1,0:T(8,128)S(1)} %bitcast.14), custom_call_target="tpu_custom_call" | custom-call | tf_op jit(solution)/shard_map/pallas_call | solution.py:249
  45.5 0.1 convert.3
  45.5 0.0 copy-done.2
  45.5 0.0 copy-done.3
  45.6 2.3 %broadcast_select_fusion = (bf16[2,2,68,768]{3,1,2,0:T(2,128)(2,1)}, bf16[2,2,68,768]{3,1,2,0:T(2,128)(2,1)}, bf16[2,2,68,768]{3,1,2,0:T(2,128)(2,1)}) fusion(pred[2,768]{1,0:T(4,128)(4,1)S(1)} %iota_compare_fusion.1, f32[2,2,68,768]{3,2,1,0:T(8,128)S(1)} %convert.3, bf16[2,2,68,768]{3,1,2,0:T(2,128)(2,1)S(1)} %copy-done.2, ...), kind=kLoop, calls=%fused_computation.3 | loop fusion | flops 1880064 | bytes 3552768 | tf_op jit(solution)/shard_map/jit(_where)/select_n | solution.py:314
  (5 shorter events, 0.1 us)
Async XLA Ops:
  0.6 2.9 %copy-start.1 = (bf16[2,2,68,768]{3,1,2,0:T(2,128)(2,1)S(1)}, bf16[2,2,68,768]{3,1,2,0:T(2,128)(2,1)}, u32[]{:S(2)}) copy-start(bf16[2,2,68,768]{3,1,2,0:T(2,128)(2,1)} %param.8) | copy-start | bytes 1253380
  3.1 1.4 %copy-start = (bf16[1,24,136,136]{3,2,1,0:T(8,128)(2,1)S(1)}, bf16[1,24,136,136]{3,2,1,0:T(8,128)(2,1)}, u32[]{:S(2)}) copy-start(bf16[1,24,136,136]{3,2,1,0:T(8,128)(2,1)} %param.10) | copy-start | bytes 2663428
  4.6 41.0 %copy-start.2 = (bf16[2,2,68,768]{3,1,2,0:T(2,128)(2,1)S(1)}, bf16[2,2,68,768]{3,1,2,0:T(2,128)(2,1)}, u32[]{:S(2)}) copy-start(bf16[2,2,68,768]{3,1,2,0:T(2,128)(2,1)} %param.9) | copy-start | bytes 1253380
  4.6 41.0 %copy-start.3 = (bf16[2,2,68,768]{3,1,2,0:T(2,128)(2,1)S(1)}, bf16[2,2,68,768]{3,1,2,0:T(2,128)(2,1)}, u32[]{:S(2)}) copy-start(bf16[2,2,68,768]{3,1,2,0:T(2,128)(2,1)} %param.7) | copy-start | bytes 1253380

commit v4 on v3

--- a/solution.py
+++ b/solution.py
@@ -53,8 +53,9 @@
 
 
 def chunk_rows(flat_rows):
-    size = max(1, flat_rows // 2)
-    return [range(r, min(r + size, flat_rows)) for r in range(0, flat_rows, size)]
+    size = max(1, flat_rows // 4)
+    cuts = [0, size, flat_rows - size, flat_rows]
+    return [range(lo, hi) for lo, hi in zip(cuts, cuts[1:]) if hi > lo]
 
 
 def exchange_kernel(wave_count, lev_count, chunks, source, matrices, proj, solved_out, coupled_out, *scratch):
@@ -73,7 +74,7 @@
     groups = local_n // 8
     layer_count = lev_local * lev_count
     extra = layer_count - LANES
-    wave_peers = [lax.rem(wave + s, wave_count) for s in range(1, wave_count)]
+    wave_peers = [lax.rem(wave + s, wave_count) for s in sorted(range(1, wave_count), key=lambda s: abs(2 * s - wave_count))]
     lev_peers = [lax.rem(lev + s, lev_count) for s in range(1, lev_count)]
 
     barrier = pltpu.get_barrier_semaphore()
@@ -190,7 +191,7 @@
             strided[size, rows, :] = rest
             return carry
 
-        lax.fori_loop(0, local_n, solve, 0, unroll=4)
+        lax.fori_loop(0, local_n, solve, 0, unroll=8)
         returning[c][...] = pack([strided[i] for i in range(size)], strided[size], size * extra)
         back_copies.append(exchange(returning, returned, back_send, back_recv, c))
 

time: 48.5 us -> 47.1 us (0.971)
  Pallas kernels: 40.9 us -> 40 us
    pallas_call x1, Pallas kernels: 40.9 us -> 40 us  [exchange_by_kernel(): pl.pallas_call(functools.partial(exchange_kernel, wave_count, lev_count,...]
where the time goes in v4:
time: 47.1 us; the launch traced here: 46.9 us
  Pallas kernels  40 us (85%)
  other arithmetic  4.09 us (9%)
  local copies, waits for them, and re-layouts  2.07 us (4%)
  between operations  0.75 us (2%)
    pallas_call x1, Pallas kernels, exchange_by_kernel(): pl.pallas_call(functools.partial(exchange_kernel, wave_count, lev_count,...  40 us
    select_n x1, other arithmetic, on_device(): jnp.where(interior_slice, heat_updated, empty_placeholder)  2.26 us
    unnamed x10, local copies, waits for them, and re-layouts  1.15 us

profile of v4, /device:TPU:0, one launch (start us, length us, event | category | flops | bytes accessed | tf_op | source)
XLA Modules:
  0.0 46.9 jit_solution(660247134182127743)
XLA Ops:
  0.6 0.0 copy-start.1
  0.6 0.8 %dynamic_slice.3 = f32[68]{0:T(128)S(1)} dynamic-slice(f32[136]{0:T(256)} %param.12, s32[]{:T(128)S(6)} %select_n.13), dynamic_slice_sizes={68} | dynamic-slice | bytes 548 | tf_op jit(solution)/shard_map/dynamic_slice | solution.py:306
  1.4 0.7 %iota_compare_fusion.1 = pred[2,768]{1,0:T(4,128)(4,1)S(1)} fusion(s32[2]{0:T(128)} %param.13), kind=kLoop, calls=%fused_computation.12 | loop fusion | flops 1536 | bytes 1544 | tf_op jit(solution)/shard_map/ge | solution.py:310
  2.2 0.9 %bitcast_convert_fusion = f32[1,136,136]{2,1,0:T(8,128)S(1)} fusion(bf16[136,136]{1,0:T(8,128)(2,1)} %param.11), kind=kLoop, calls=%fused_computation.10 | loop fusion | flops 18496 | bytes 110976 | tf_op jit(solution)/shard_map/stack | solution.py:239
  3.1 0.0 copy-start
  3.1 0.1 copy.19
  3.3 0.1 pad.4.clone
  3.4 0.1 add_divide_fusion
  3.5 0.0 copy-done.1
  3.6 0.9 %copy-done = bf16[1,24,136,136]{3,2,1,0:T(8,128)(2,1)S(1)} copy-done((bf16[1,24,136,136]{3,2,1,0:T(8,128)(2,1)S(1)}, bf16[1,24,136,136]{3,2,1,0:T(8,128)(2,1)}, u32[]{:S(2)}) %copy-start) | copy-done | bytes 887832
  4.6 0.0 copy-start.2
  4.6 0.0 copy-start.3
  4.6 40.0 %shard_map.94 = (bf16[4,68,768]{2,1,0:T(8,128)(2,1)S(1)}, bf16[4,68,768]{2,1,0:T(8,128)(2,1)S(1)}) custom-call(bf16[4,68,768]{2,1,0:T(8,128)(2,1)S(1)} %bitcast.12, bf16[24,136,136]{2,1,0:T(8,128)(2,1)S(1)} %bitcast.13, f32[4,68,256]{2,1,0:T(8,128)S(1)} %bitcast.14), custom_call_target="tpu_custom_call" | custom-call | tf_op jit(solution)/shard_map/pallas_call | solution.py:250
  44.5 0.1 convert.3
  44.6 0.0 copy-done.2
  44.6 0.0 copy-done.3
  44.6 2.3 %broadcast_select_fusion = (bf16[2,2,68,768]{3,1,2,0:T(2,128)(2,1)}, bf16[2,2,68,768]{3,1,2,0:T(2,128)(2,1)}, bf16[2,2,68,768]{3,1,2,0:T(2,128)(2,1)}) fusion(pred[2,768]{1,0:T(4,128)(4,1)S(1)} %iota_compare_fusion.1, f32[2,2,68,768]{3,2,1,0:T(8,128)S(1)} %convert.3, bf16[2,2,68,768]{3,1,2,0:T(2,128)(2,1)S(1)} %copy-done.2, ...), kind=kLoop, calls=%fused_computation.3 | loop fusion | flops 1880064 | bytes 3552768 | tf_op jit(solution)/shard_map/jit(_where)/select_n | solution.py:315
  (5 shorter events, 0.1 us)
Async XLA Ops:
  0.6 2.9 %copy-start.1 = (bf16[2,2,68,768]{3,1,2,0:T(2,128)(2,1)S(1)}, bf16[2,2,68,768]{3,1,2,0:T(2,128)(2,1)}, u32[]{:S(2)}) copy-start(bf16[2,2,68,768]{3,1,2,0:T(2,128)(2,1)} %param.8) | copy-start | bytes 1253380
  3.1 1.4 %copy-start = (bf16[1,24,136,136]{3,2,1,0:T(8,128)(2,1)S(1)}, bf16[1,24,136,136]{3,2,1,0:T(8,128)(2,1)}, u32[]{:S(2)}) copy-start(bf16[1,24,136,136]{3,2,1,0:T(8,128)(2,1)} %param.10) | copy-start | bytes 2663428
  4.6 40.0 %copy-start.2 = (bf16[2,2,68,768]{3,1,2,0:T(2,128)(2,1)S(1)}, bf16[2,2,68,768]{3,1,2,0:T(2,128)(2,1)}, u32[]{:S(2)}) copy-start(bf16[2,2,68,768]{3,1,2,0:T(2,128)(2,1)} %param.9) | copy-start | bytes 1253380
  4.6 40.1 %copy-start.3 = (bf16[2,2,68,768]{3,1,2,0:T(2,128)(2,1)S(1)}, bf16[2,2,68,768]{3,1,2,0:T(2,128)(2,1)}, u32[]{:S(2)}) copy-start(bf16[2,2,68,768]{3,1,2,0:T(2,128)(2,1)} %param.7) | copy-start | bytes 1253380
